TPU v7x, 32 devices: a whole 2x2x4 slice. The times are simulated.
32 devices in a mesh: req: 8 (over y, x, core), head: 4 (over z).
Axes of the slice: x: 2, y: 2, z: 4, core: 2. Of those that a mesh axis runs over, the one named last changes fastest.
Arguments:
- queries: bfloat16 [128, 64, 128], P('req', 'head'), may hold values from -6 to 6
- k_codes: bfloat16 [8192, 16, 8, 128], P('req', None, 'head'), may hold values from -6 to 6
- value_quantized_codes: bfloat16 [8192, 16, 8, 128], P('req', None, 'head'), may hold values from -6 to 6
- key_page_scale: float32 [8192, 8], P('req', 'head'), may hold values from 0.5 to 2
- value_page_scale: float32 [8192, 8], P('req', 'head'), may hold values from 4 to 16
- lengths: int32 [128], P('req'), may hold values from 1 to 2032
- page_table: int32 [128, 128], P('req'), may hold values from -1 to 8191, as said below
- out_weight: bfloat16 [8192, 8192], P('head', 'req'), may hold values from -0.0625 to 0.0625
Outputs:
- attn_out: bfloat16 [128, 8192], P(None, ('req', 'head'))
Inputs may be any that keep to these rules, and one draw needn't show every extreme that they name: `page_table`: entries j below ceil(lengths[r] / 16) name pool pages; all such entries of all requests together name every pool page exactly once. Entries beyond are -1.
All inputs are finite; a program needn't handle non-finite values.
Results may differ from a plain program's by a relative error of at most 0.02.
Values may be sent and summed in bfloat16 or wider, within the bound.
No kernel may reach another device: no remote copies, remote signals or barrier semaphores. Data moves between devices by JAX's collectives and lax.ppermute only.
A program may use at most 128 MiB of HBM per device.

v0:
```python
import math

import jax
import jax.numpy as jnp
from jax import lax
from jax.sharding import PartitionSpec as P

floor_score = -1e30


def split_product(member_b, data):
    high_part = data.astype(jnp.bfloat16)
    low_part = (data - high_part.astype(jnp.float32)).astype(jnp.bfloat16)
    first = jnp.dot(member_b, high_part, preferred_element_type=jnp.float32)
    return first + jnp.dot(member_b, low_part, preferred_element_type=jnp.float32)


def locate_pages(all_table, all_lengths, offset, pages_here):
    request_count, table_width = all_table.shape
    flat_ids = all_table.reshape(request_count * table_width)
    local_slot = flat_ids - offset
    inside = (flat_ids >= 0) & (local_slot >= 0) & (local_slot < pages_here)
    target = jnp.where(inside, local_slot, pages_here)
    entry_code = jnp.arange(request_count * table_width, dtype=jnp.int32)
    placed = jnp.zeros((pages_here,), jnp.int32).at[target].set(entry_code, mode="drop")
    owners = placed // table_width
    ranks = placed % table_width
    return (owners, ranks, all_lengths[owners])


def on_device(
    queries,
    k_codes,
    value_quantized_codes,
    key_page_scale,
    value_page_scale,
    lengths,
    page_table,
    out_weight,
):
    pages_here, page_size, kv_local, head_size = k_codes.shape
    rows_here = queries.shape[0]
    heads_local = queries.shape[1]
    query_group_count = heads_local // kv_local
    every_query = lax.all_gather(queries, "req", axis=0, tiled=True)
    all_lengths, all_table = (
        lax.all_gather(lengths, "req", axis=0, tiled=True),
        lax.all_gather(page_table, "req", axis=0, tiled=True),
    )
    request_count, table_width = all_table.shape
    offset = lax.axis_index("req") * pages_here
    owners, page_rank, page_length = locate_pages(all_table, all_lengths, offset, pages_here)
    position = page_rank[:, None] * page_size + jnp.arange(page_size, dtype=jnp.int32)[None, :]
    is_live = (position < page_length[:, None])[:, None, None, :]
    page_query = every_query[owners].reshape(pages_here, kv_local, query_group_count, head_size)
    scores = jnp.einsum("pkgd,ptkd->pkgt", page_query, k_codes, preferred_element_type=jnp.float32)
    scores = scores * (key_page_scale[:, :, None, None] / math.sqrt(head_size))
    page_max = jnp.max(jnp.where(is_live, scores, floor_score), axis=-1)
    weights = jnp.where(is_live, jnp.exp(scores - page_max[..., None]), 0.0).astype(jnp.bfloat16)
    page_sum = jnp.sum(weights.astype(jnp.float32), axis=-1).reshape(pages_here, heads_local)
    page_out = jnp.einsum(
        "pkgt,ptkd->pkgd", weights, value_quantized_codes, preferred_element_type=jnp.float32
    )
    page_out = (page_out * value_page_scale[:, :, None, None]).reshape(
        pages_here, heads_local, head_size
    )
    page_max = page_max.reshape(pages_here, heads_local)
    member = owners[:, None] == jnp.arange(request_count, dtype=jnp.int32)[None, :]
    local_peak = jnp.max(jnp.where(member[:, :, None], page_max[:, None, :], floor_score), axis=0)
    member_b = member.astype(jnp.bfloat16).T
    factor = jnp.exp(page_max - local_peak[owners])
    weighted = (page_out * factor[:, :, None]).reshape(pages_here, heads_local * head_size)
    numerator = split_product(member_b, weighted)
    denominator = split_product(member_b, page_sum * factor)
    numerator, denominator = (numerator, denominator)
    sources = lax.axis_size("req")
    numer_in = lax.all_to_all(
        numerator.reshape(sources, rows_here, heads_local * head_size),
        "req",
        split_axis=0,
        concat_axis=0,
        tiled=True,
    )
    denom_in = lax.all_to_all(
        denominator.reshape(sources, rows_here, heads_local),
        "req",
        split_axis=0,
        concat_axis=0,
        tiled=True,
    )
    peak_in = lax.all_to_all(
        local_peak.reshape(sources, rows_here, heads_local),
        "req",
        split_axis=0,
        concat_axis=0,
        tiled=True,
    )
    row_count = numer_in.shape[1]
    overall = jnp.max(peak_in, axis=0)
    factor = jnp.exp(peak_in - overall[None])
    numer_sum = jnp.sum(
        numer_in.reshape(sources, row_count, heads_local, head_size) * factor[..., None], axis=0
    )
    denom_sum = jnp.sum(denom_in * factor, axis=0)
    attention = (numer_sum / denom_sum[..., None]).reshape(row_count, heads_local * head_size)
    attention = attention.astype(jnp.bfloat16)
    terms = jnp.dot(
        lax.all_gather(attention, "req", axis=0, tiled=True),
        out_weight,
        preferred_element_type=jnp.float32,
    )
    return lax.psum_scatter(terms.astype(jnp.bfloat16), "head", scatter_dimension=1, tiled=True)


def solution(mesh):
    in_specs = (
        P("req", "head", None),
        P("req", None, "head", None),
        P("req", None, "head", None),
        P("req", "head"),
        P("req", "head"),
        P("req"),
        P("req", None),
        P("head", "req"),
    )
    out_specs = P(None, ("req", "head"))
    return jax.shard_map(
        on_device, mesh=mesh, in_specs=in_specs, out_specs=out_specs, check_vma=False
    )
```

profile of v0, /device:TPU:0, one launch (start us, length us, event | category | flops | bytes accessed | tf_op | source)
XLA Modules:
  0.0 246.5 jit_solution(17993828565912308326)
XLA Ops:
  6.5 1.2 dynamic-slice
  8.4 0.9 dynamic-update-slice
  9.3 9.5 %all-reduce = s32[128]{0:T(128)S(1)} all-reduce(s32[128]{0:T(128)S(1)} %dynamic-update-slice), channel_id=1, replica_groups=mesh['req'=8,'head'=4] {'req'}, use_global_device_ids=true, to_apply=%add | all-reduce | flops 128 | bytes 1024
  18.8 0.7 broadcast_multiply_fusion.1
  19.5 8.6 %all_gather.12 = s32[128,128]{1,0:T(8,128)S(1)} all-gather(s32[16,128]{1,0:T(8,128)} %param.14), channel_id=1, replica_groups=mesh['req'=8,'head'=4] {'req'}, dimensions={0}, use_global_device_ids=true | all-gather | bytes 73728 | tf_op jit(solution)/shard_map/all_gather | solution.py:48
  28.3 60.3 %scatter_custom_fusion = s32[1024]{0:T(1024)S(1)} fusion(s32[16384]{0:T(1024)S(1)} %bitcast.101, s32[16384]{0:T(1024)S(1)} %iota.18, s32[]{:T(128)} %constant.37.clone.1), kind=kCustom, calls=%fused_computation.56 | custom fusion | bytes 4100 | tf_op jit(solution)/shard_map/scatter | solution.py:25
  89.1 9.5 %all_gather.14 = bf16[128,16,128]{2,1,0:T(8,128)(2,1)S(1)} all-gather(bf16[16,16,128]{2,1,0:T(8,128)(2,1)} %param.8), channel_id=1, replica_groups=mesh['req'=8,'head'=4] {'req'}, dimensions={0}, use_global_device_ids=true | all-gather | bytes 589824 | tf_op jit(solution)/shard_map/all_gather | solution.py:45
  98.6 6.6 %gather_fusion = s32[1024]{0:T(1024)S(1)} fusion(s32[128]{0:T(128)S(1)} %all-reduce, s32[1024]{0:T(1024)S(1)} %get-tuple-element.7), kind=kCustom, calls=%fused_computation | custom fusion | bytes 12288 | tf_op jit(solution)/shard_map/gather | solution.py:28
  105.2 8.5 %gather_fusion.1 = bf16[1024,16,128]{2,1,0:T(8,128)(2,1)} fusion(bf16[128,16,128]{2,1,0:T(8,128)(2,1)S(1)} %all_gather.14, s32[1024]{0:T(1024)S(1)} %get-tuple-element.7), kind=kCustom, calls=%fused_computation.1 | custom fusion | bytes 8392704 | tf_op jit(solution)/shard_map/gather | solution.py:55
  114.0 10.4 %select_reduce_fusion.1 = (f32[1024,2,8]{2,1,0:T(2,128)S(1)}, f32[1024,2,8,16]{3,2,1,0:T(8,128)}) fusion(f32[1024,2]{1,0:T(8,128)S(1)} %copy.55, pred[1024,16]{1,0:T(8,128)(4,1)S(1)} %add_compare_fusion, bf16[1024,16,2,128]{3,2,1,0:T(2,128)(2,1)} %param.9, bf16[1024,16,128]{2,1,0:T(8,128)(2,1)} %gather_fusion.1), kind=kOutput, calls=%fused_computation.13 | convolution fusion | flops 67878912 | bytes 13721600 | tf_op jit(solution)/shard_map/pkgd,ptkd->pkgt/dot_general | solution.py:56
  124.4 0.4 copy.58
  125.0 5.2 %select_reduce_fusion = f32[128,16]{0,1:T(8,128)S(1)} fusion(f32[1024,16]{1,0:T(8,128)S(1)} %copy.59, pred[1024,128]{1,0:T(8,128)(4,1)S(1)} %iota_compare_fusion), kind=kLoop, calls=%fused_computation.11 | loop fusion | flops 4192256 | bytes 204800 | tf_op jit(solution)/shard_map/reduce_max | solution.py:69
  130.4 0.7 reshape.194
  131.1 3.5 %all-to-all-start.1 = ((f32[8,1,256]{2,1,0:T(1,128)}), f32[8,1,256]{2,1,0:T(1,128)S(1)}, u32[]{:S(2)}, u32[]{:S(2)}) async-start(f32[8,1,256]{2,1,0:T(1,128)} %reshape.194), calls=%async_computation.1 | async-start | bytes 16384 | tf_op jit(solution)/shard_map/all_to_all | solution.py:91
  134.7 1.1 copy.57
  135.8 2.8 %gather_fusion.2 = f32[1024,16]{1,0:T(8,128)S(1)} fusion(f32[128,16]{1,0:T(8,128)S(1)} %copy.60, s32[1024]{0:T(1024)S(1)} %get-tuple-element.7), kind=kCustom, calls=%fused_computation.2 | custom fusion | bytes 135168 | tf_op jit(solution)/shard_map/gather | solution.py:71
  139.0 9.6 %convert_reduce_fusion = f32[1024,2,8]{2,1,0:T(2,128)S(1)} fusion(f32[1024,2,8]{2,1,0:T(2,128)S(1)} %get-tuple-element.10, f32[1024,2,8,16]{3,2,1,0:T(8,128)} %get-tuple-element.11, f32[1024,2]{1,0:T(8,128)S(1)} %copy.55, pred[1024,16]{1,0:T(8,128)(4,1)S(1)} %add_compare_fusion), kind=kLoop, calls=%fused_computation.9 | loop fusion | flops 1556480 | bytes 1204224 | tf_op jit(solution)/shard_map/reduce_sum | solution.py:60
  148.6 0.4 copy.65
  149.3 11.1 %broadcast_multiply_fusion = f32[1024,2,8,128]{3,2,1,0:T(8,128)S(1)} fusion(f32[1024,2]{1,0:T(8,128)} %copy.57, bf16[1024,16,2,128]{3,2,1,0:T(2,128)(2,1)} %param.10, f32[1024,2,8,16]{3,2,1,0:T(8,128)} %get-tuple-element.11, f32[1024,2,8]{2,1,0:T(2,128)S(1)} %get-tuple-element.10, f32[1024,2]{1,0:T(8,128)S(1)} %copy.55, ...), kind=kOutput, calls=%fused_computation.16 | convolution fusion | flops 70254592 | bytes 17924096 | tf_op jit(solution)/shard_map/pkgt,ptkd->pkgd/dot_general | solution.py:61
  160.5 2.3 mul.61
  162.8 4.8 %fusion.10 = f32[128,2048]{1,0:T(8,128)S(1)} fusion(f32[128,8,16,128]{3,2,1,0:T(8,128)S(1)} %bitcast.92, f32[128,8,16,128]{3,2,1,0:T(8,128)S(1)} %bitcast.94, s32[1024]{0:T(1024)S(1)} %get-tuple-element.8), kind=kOutput, calls=%fused_computation.18 | convolution fusion | flops 541196288 | bytes 17829888 | tf_op jit(solution)/shard_map/dot_general | solution.py:14
  168.0 0.7 reshape.196
  168.7 4.0 %all-to-all-start.2 = ((f32[8,1,256]{2,1,0:T(1,128)}), f32[8,1,256]{2,1,0:T(1,128)S(1)}, u32[]{:S(2)}, u32[]{:S(2)}) async-start(f32[8,1,256]{2,1,0:T(1,128)} %reshape.196), calls=%async_computation.2 | async-start | bytes 16384 | tf_op jit(solution)/shard_map/all_to_all | solution.py:84
  172.7 14.2 %fusion.12 = f32[128,2048]{1,0:T(8,128)} fusion(f32[128,2048]{1,0:T(8,128)S(1)} %fusion.10, f32[128,8,16,128]{3,2,1,0:T(8,128)} %bitcast.93, f32[128,8,16,128]{3,2,1,0:T(8,128)} %bitcast.95, s32[1024]{0:T(1024)S(1)} %get-tuple-element.8), kind=kOutput, calls=%fused_computation.19 | convolution fusion | flops 547749888 | bytes 18878464 | tf_op jit(solution)/shard_map/dot_general | solution.py:15
  186.8 4.2 %all-to-all-start = ((f32[8,16,2048]{2,1,0:T(8,128)}), f32[8,16,2048]{2,1,0:T(8,128)S(1)}, u32[]{:S(2)}, u32[]{:S(2)}) async-start(f32[8,16,2048]{2,1,0:T(8,128)} %bitcast.5), calls=%async_computation | async-start | bytes 2097152 | tf_op jit(solution)/shard_map/all_to_all | solution.py:77
  191.1 0.5 broadcast.139
  191.6 0.7 reduce.1
  192.3 0.7 reduce.2
  193.8 12.6 %all-to-all-done = f32[8,16,2048]{2,1,0:T(8,128)S(1)} async-done(((f32[8,16,2048]{2,1,0:T(8,128)}), f32[8,16,2048]{2,1,0:T(8,128)S(1)}, u32[]{:S(2)}, u32[]{:S(2)}) %all-to-all-start) | async-done | bytes 1048608 | tf_op jit(solution)/shard_map/all_to_all | solution.py:77
  206.7 8.9 %all_gather.15 = bf16[128,2048]{1,0:T(8,128)(2,1)S(1)} all-gather(bf16[16,2048]{1,0:T(8,128)(2,1)S(1)} %fusion.20), channel_id=1, replica_groups=mesh['req'=8,'head'=4] {'req'}, dimensions={0}, use_global_device_ids=true | all-gather | bytes 589824 | tf_op jit(solution)/shard_map/all_gather | solution.py:108
  215.6 3.6 %convolution_convert_fusion = bf16[128,1024]{1,0:T(8,128)(2,1)} fusion(bf16[128,2048]{1,0:T(8,128)(2,1)S(1)} %all_gather.15, bf16[2048,1024]{1,0:T(8,128)(2,1)} %param.15), kind=kOutput, calls=%fused_computation.20 | convolution fusion | flops 537001984 | bytes 4980736 | tf_op jit(solution)/shard_map/dot_general | solution.py:107
  219.2 20.4 %reduce-scatter.2.cloned.1.call-done = bf16[128,256]{1,0:T(8,128)(2,1)} async-done(((bf16[128,1024]{1,0:T(8,128)(2,1)}), bf16[128,256]{1,0:T(8,128)(2,1)}) %reduce-scatter.2.cloned.1.call-update) | async-done | bytes 65552 | tf_op jit(solution)/shard_map/reduce_scatter | solution.py:112
  (41 shorter events, 3.7 us)
Async XLA Ops:
  114.0 20.7 %copy-start.2 = (f32[1024,2]{0,1:T(2,128)S(1)}, f32[1024,2]{0,1:T(2,128)}, u32[]{:S(2)}) copy-start(f32[1024,2]{0,1:T(2,128)} %param.12) | copy-start | bytes 24580
  131.1 37.7 %all-to-all-start.1 = ((f32[8,1,256]{2,1,0:T(1,128)}), f32[8,1,256]{2,1,0:T(1,128)S(1)}, u32[]{:S(2)}, u32[]{:S(2)}) async-start(f32[8,1,256]{2,1,0:T(1,128)} %reshape.194), calls=%async_computation.1 | async-start | bytes 16384 | tf_op jit(solution)/shard_map/all_to_all | solution.py:91
  160.4 7.1 %copy-start.1 = (f32[1024,2,8,128]{3,2,1,0:T(8,128)}, f32[1024,2,8,128]{3,2,1,0:T(8,128)S(1)}, u32[]{:S(2)}) copy-start(f32[1024,2,8,128]{3,2,1,0:T(8,128)S(1)} %broadcast_multiply_fusion) | copy-start | bytes 25165828
  162.8 4.8 %copy-start = (f32[1024,16,128]{2,1,0:T(8,128)}, f32[1024,16,128]{2,1,0:T(8,128)S(1)}, u32[]{:S(2)}) copy-start(f32[1024,16,128]{2,1,0:T(8,128)S(1)} %mul.61) | copy-start | bytes 25165828
  168.7 18.1 %all-to-all-start.2 = ((f32[8,1,256]{2,1,0:T(1,128)}), f32[8,1,256]{2,1,0:T(1,128)S(1)}, u32[]{:S(2)}, u32[]{:S(2)}) async-start(f32[8,1,256]{2,1,0:T(1,128)} %reshape.196), calls=%async_computation.2 | async-start | bytes 16384 | tf_op jit(solution)/shard_map/all_to_all | solution.py:84
  186.8 19.6 %all-to-all-start = ((f32[8,16,2048]{2,1,0:T(8,128)}), f32[8,16,2048]{2,1,0:T(8,128)S(1)}, u32[]{:S(2)}, u32[]{:S(2)}) async-start(f32[8,16,2048]{2,1,0:T(8,128)} %bitcast.5), calls=%async_computation | async-start | bytes 2097152 | tf_op jit(solution)/shard_map/all_to_all | solution.py:77
  191.0 48.7 %reduce-scatter.2.cloned.1.call-start = ((), (), s32[]{:S(2)}) async-start(), calls=%async_computation.4 | async-start | bytes 327680 | tf_op jit(solution)/shard_map/reduce_scatter | solution.py:112
Sparse Core Ops, SparseCore 0:
  219.3 20.2 reduce-scatter.1
where the time goes:
time: 247 us
  local copies, waits for them, and re-layouts  88.3 us (36%)
  matrix products  44.7 us (18%)
  blocking collectives  36.5 us (15%)
  waiting for transfers between devices  33.1 us (13%)
  other arithmetic  17.9 us (7%)
  between operations  14.4 us (6%)
  starting transfers between devices  11.7 us (5%)
    scatter x1, local copies, waits for them, and re-layouts, locate_pages(): jnp.zeros((pages_here,), jnp.int32).at[target].set(entry_code, mode='drop')  60.3 us
    reduce_scatter x1, waiting for transfers between devices, on_device(): lax.psum_scatter(terms.astype(jnp.bfloat16), 'head', scatter_dimension=1,...  20.4 us
    dot_general x2, matrix products, split_product(): jnp.dot(member_b, low_part, preferred_element_type=jnp.float32)  14.5 us
    all_to_all x1, waiting for transfers between devices, on_device(): lax.all_to_all(numerator.reshape(sources, rows_here, heads_local * head_s...  12.6 us
    dot_general x1, matrix products, on_device(): jnp.einsum('pkgt,ptkd->pkgd', weights, value_quantized_codes, preferred_e...  11.1 us
    dot_general x1, matrix products, on_device(): jnp.einsum('pkgd,ptkd->pkgt', page_query, k_codes, preferred_element_type...  10.4 us
    reduce_sum x1, other arithmetic, on_device(): jnp.sum(weights.astype(jnp.float32), axis=-1)  9.62 us
    all_gather x1, blocking collectives, on_device(): every_query = lax.all_gather(queries, 'req', axis=0, tiled=True)  9.51 us
  transfers between devices with their start and end apart: 4, of which 2 were waited for; matrix products, arithmetic and copies ran while one was open for 21% of the time, Pallas kernels for 0%

commit v1 on v0

v1 whole, which is shorter than its diff:
```python
import functools
import math

import jax
import jax.numpy as jnp
from jax import lax
from jax.experimental import pallas as pl
from jax.experimental.pallas import tpu as pltpu
from jax.sharding import PartitionSpec as P

floor_score = float(jnp.bfloat16(-1e30))
LANES = 128
GROUP = 8
BLOCK = 256


def place_pages(gath_ref, offset, pages, width, tokens, placed_ref):
    requests = gath_ref.shape[0]
    page_rows = pages // LANES
    chunk = 16
    entry = lax.broadcasted_iota(jnp.int32, (chunk, LANES), 1).astype(jnp.float32)
    line = lax.broadcasted_iota(jnp.int32, (chunk, LANES), 0)
    sub = lax.broadcasted_iota(jnp.int32, (LANES, LANES), 0)
    sub_row = lax.broadcasted_iota(jnp.int32, (page_rows, LANES), 0)

    def step(c, total):
        rows = pl.ds(pl.multiple_of(c * chunk, chunk), chunk)
        high = gath_ref[rows, width : width + LANES].astype(jnp.float32)
        low = gath_ref[rows, width + LANES : width + 2 * LANES].astype(jnp.float32)
        lens = gath_ref[rows, width + 2 * LANES : width + 3 * LANES].astype(jnp.float32)
        length = lens[:, 0:1] * 256.0 + lens[:, 1:2]
        slot = (high * 256.0 + low).astype(jnp.int32) - offset
        inside = (slot >= 0) & (slot < pages)
        slot_row = jnp.where(inside, slot >> 7, -1)
        slot_lane = slot & (LANES - 1)
        live = jnp.clip(length - entry * float(tokens), 0.0, float(tokens))
        owner = c * chunk + line
        owner_high = (owner >> 7).astype(jnp.float32)
        owner_low = (owner & (LANES - 1)).astype(jnp.float32)
        lefts, rights = [], []
        for i in range(chunk):
            here = sub_row == slot_row[i : i + 1]
            parts = [
                jnp.where(here, v[i : i + 1], 0.0) for v in (owner_high, owner_low, live, live)
            ]
            lefts.append(jnp.concatenate(parts, axis=0).astype(jnp.bfloat16))
            rights.append(jnp.where(sub == slot_lane[i : i + 1], 1.0, 0.0).astype(jnp.bfloat16))
        return total + lax.dot_general(
            jnp.concatenate(lefts, axis=1),
            jnp.concatenate(rights, axis=1),
            (((1,), (1,)), ((), ())),
            preferred_element_type=jnp.float32,
        )

    start = jnp.zeros((4 * page_rows, LANES), jnp.float32)
    placed_ref[...] = lax.fori_loop(0, requests // chunk, step, start)


def attend_kernel(
    offset_ref,
    gath_ref,
    ks_ref,
    vs_ref,
    k_hbm,
    v_hbm,
    out_ref,
    k_buf,
    v_buf,
    placed_ref,
    cols_ref,
    owner_ref,
    qg_ref,
    po_ref,
    pm_ref,
    pmt_ref,
    acc_ref,
    m_ref,
    sems,
    *,
    heads,
    kv,
    tokens,
):
    requests = gath_ref.shape[0]
    width = heads * LANES
    pages = ks_ref.shape[1]
    blocks = pages // BLOCK
    page_rows = pages // LANES
    halves = BLOCK // LANES
    block_rows = BLOCK * tokens * kv
    group_rows = GROUP * tokens * kv
    per_kv = heads // kv

    def copies(b):
        rows = pl.ds(b * block_rows, block_rows)
        return (
            pltpu.make_async_copy(k_hbm.at[rows], k_buf.at[rows], sems.at[0, b]),
            pltpu.make_async_copy(v_hbm.at[rows], v_buf.at[rows], sems.at[1, b]),
        )

    for b in range(blocks):
        for copy in copies(b):
            copy.start()

    place_pages(gath_ref, offset_ref[0], pages, width, tokens, placed_ref)
    acc_ref[...] = jnp.zeros(acc_ref.shape, jnp.float32)
    m_ref[...] = jnp.full(m_ref.shape, floor_score, jnp.float32)

    col = lax.broadcasted_iota(jnp.int32, (GROUP, group_rows), 1)
    row = lax.broadcasted_iota(jnp.int32, (GROUP, group_rows), 0)
    token = (col % (tokens * kv)) // kv
    keys = [
        jnp.where((col // (tokens * kv) == row) & (col % kv == k), token, 2 * tokens).astype(
            jnp.float32
        )
        for k in range(kv)
    ]
    lane = lax.broadcasted_iota(jnp.int32, (GROUP, LANES), 1)
    sub8 = lax.broadcasted_iota(jnp.int32, (8, LANES), 0)
    lane_r = lax.broadcasted_iota(jnp.int32, (BLOCK, requests), 1).astype(jnp.float32)
    sub_r = lax.broadcasted_iota(jnp.int32, (requests, BLOCK), 0).astype(jnp.float32)
    ones = jnp.ones((group_rows, LANES), jnp.bfloat16)

    def block_step(b, carry):
        for u in range(halves):
            at = b * halves + u
            owner = placed_ref[pl.ds(at, 1), :] * 128.0 + placed_ref[pl.ds(page_rows + at, 1), :]
            live = placed_ref[pl.ds(2 * page_rows + at, 1), :]
            span = pl.ds(pl.multiple_of(at * LANES, LANES), LANES)
            rows = [owner, live]
            rows += [ks_ref[k : k + 1, span] * (1.0 / math.sqrt(LANES)) for k in range(kv)]
            rows += [vs_ref[k : k + 1, span] for k in range(kv)]
            stacked = jnp.zeros((8, LANES), jnp.float32)
            for i, r in enumerate(rows):
                stacked = jnp.where(sub8 == i, r, stacked)
            full = jnp.concatenate([stacked, jnp.zeros((LANES - 8, LANES), jnp.float32)], axis=0)
            cols_ref[u * LANES : (u + 1) * LANES, :] = full.T
            owner_ref[0:1, u * LANES : (u + 1) * LANES] = owner
        member_t = jnp.where(cols_ref[:, 0:1] == lane_r, 1.0, 0.0).astype(jnp.bfloat16)
        for h in range(0, heads, 2):
            pair = jnp.dot(
                member_t,
                gath_ref[:, h * LANES : (h + 2) * LANES],
                preferred_element_type=jnp.float32,
            )
            qg_ref[h] = pair[:, :LANES]
            qg_ref[h + 1] = pair[:, LANES:]
        for copy in copies(b):
            copy.wait()

        def group_step(g, inner):
            at = pl.ds(pl.multiple_of(g * GROUP, GROUP), GROUP)
            start = pl.multiple_of(b * block_rows + g * group_rows, group_rows)
            q = qg_ref[:, at, :].reshape(heads * GROUP, LANES).astype(jnp.bfloat16)
            s = lax.dot_general(
                q,
                k_buf[pl.ds(start, group_rows), :],
                (((1,), (1,)), ((), ())),
                preferred_element_type=jnp.float32,
            ).reshape(heads, GROUP, group_rows)
            c = cols_ref[at, :]
            peaks = jnp.zeros((GROUP, LANES), jnp.float32)
            probs = []
            for k in range(kv):
                live = keys[k] < c[:, 1:2]
                scale = c[:, 2 + k : 3 + k]
                for i in range(k * per_kv, (k + 1) * per_kv):
                    sk = jnp.where(live, s[i] * scale, floor_score)
                    mx = jnp.max(sk, axis=-1, keepdims=True)
                    probs.append(jnp.exp(sk - mx))
                    peaks = jnp.where(lane == i, mx, peaks)
            p = jnp.concatenate(probs, axis=0).astype(jnp.bfloat16)
            vg = jnp.concatenate([v_buf[pl.ds(start, group_rows), :], ones], axis=1)
            o = jnp.dot(p, vg, preferred_element_type=jnp.float32)
            o = o.reshape(heads, GROUP, 2 * LANES)
            for k in range(kv):
                hs = slice(k * per_kv, (k + 1) * per_kv)
                vscale = c[:, 2 + kv + k : 3 + kv + k]
                po_ref[hs, at, :LANES] = o[hs, :, :LANES] * vscale[None]
            po_ref[:, at, LANES:] = o[:, :, LANES:]
            pm_ref[at, :] = peaks
            return inner

        lax.fori_loop(0, BLOCK // GROUP, group_step, 0, unroll=4)
        for u in range(halves):
            span = slice(u * LANES, (u + 1) * LANES)
            pmt_ref[:, span] = pm_ref[span, :].T

        def head_step(h, inner):
            pm_row = pmt_ref[pl.ds(h, 1), :]
            member = sub_r == owner_ref[0:1, :]
            block_peak = jnp.max(
                jnp.where(member, pm_row, floor_score), axis=1, keepdims=True
            )
            old = m_ref[h]
            new = jnp.maximum(old, block_peak)
            alpha = jnp.exp(old - new)
            wide = jnp.concatenate([new] * halves, axis=1)
            w = jnp.exp(jnp.where(member, pm_row - wide, floor_score)).astype(jnp.bfloat16)
            o = jnp.dot(w, po_ref[h].astype(jnp.bfloat16), preferred_element_type=jnp.float32)
            acc_ref[h] = acc_ref[h] * jnp.concatenate([alpha, alpha], axis=1) + o
            m_ref[h] = new
            return inner

        lax.fori_loop(0, heads, head_step, 0, unroll=2)
        return carry

    lax.fori_loop(0, blocks, block_step, 0)

    lane_out = lax.broadcasted_iota(jnp.int32, (requests, LANES), 1)
    aux = jnp.zeros((requests, LANES), jnp.float32)
    for h in range(heads):
        peak = m_ref[h]
        shift = peak.astype(jnp.bfloat16).astype(jnp.float32)
        factor = jnp.exp(peak - shift)
        out_ref[:, h * LANES : (h + 1) * LANES] = (acc_ref[h, :, :LANES] * factor).astype(
            jnp.bfloat16
        )
        total = acc_ref[h, :, LANES:] * factor
        total_high = total.astype(jnp.bfloat16).astype(jnp.float32)
        aux = jnp.where(lane_out == h, shift, aux)
        aux = jnp.where(lane_out == heads + h, total_high, aux)
        aux = jnp.where(lane_out == 2 * heads + h, total - total_high, aux)
    out_ref[:, width : width + LANES] = aux.astype(jnp.bfloat16)


def attend(gathered, offset, k_rows, v_rows, ks, vs, heads, kv, tokens):
    requests = gathered.shape[0]
    pages = ks.shape[1]
    f32 = jnp.float32
    vmem = pl.BlockSpec(memory_space=pltpu.VMEM)
    hbm = pl.BlockSpec(memory_space=pl.ANY)
    return pl.pallas_call(
        functools.partial(attend_kernel, heads=heads, kv=kv, tokens=tokens),
        out_shape=jax.ShapeDtypeStruct((requests, (heads + 1) * LANES), jnp.bfloat16),
        in_specs=[pl.BlockSpec(memory_space=pltpu.SMEM), vmem, vmem, vmem, hbm, hbm],
        out_specs=vmem,
        scratch_shapes=[
            pltpu.VMEM(k_rows.shape, k_rows.dtype),
            pltpu.VMEM(v_rows.shape, v_rows.dtype),
            pltpu.VMEM((4 * (pages // LANES), LANES), f32),
            pltpu.VMEM((BLOCK, LANES), f32),
            pltpu.VMEM((8, BLOCK), f32),
            pltpu.VMEM((heads, BLOCK, LANES), f32),
            pltpu.VMEM((heads, BLOCK, 2 * LANES), f32),
            pltpu.VMEM((BLOCK, LANES), f32),
            pltpu.VMEM((LANES, BLOCK), f32),
            pltpu.VMEM((heads, requests, 2 * LANES), f32),
            pltpu.VMEM((heads, requests, LANES), f32),
            pltpu.SemaphoreType.DMA((2, pages // BLOCK)),
        ],
        compiler_params=pltpu.CompilerParams(vmem_limit_bytes=60 * 1024 * 1024),
        name="attend",
    )(offset, gathered, ks, vs, k_rows, v_rows)


def combine_kernel(in_ref, out_ref, *, heads):
    sources = in_ref.shape[0]
    width = heads * LANES
    aux = in_ref[:, :, width:].astype(jnp.float32)
    shift = aux[:, :, :heads]
    total = aux[:, :, heads : 2 * heads] + aux[:, :, 2 * heads : 3 * heads]
    factor = jnp.exp(shift - jnp.max(shift, axis=0, keepdims=True))
    factor = factor / jnp.sum(total * factor, axis=0, keepdims=True)
    for h in range(heads):
        span = slice(h * LANES, (h + 1) * LANES)
        value = in_ref[0, :, span].astype(jnp.float32) * factor[0, :, h : h + 1]
        for s in range(1, sources):
            value += in_ref[s, :, span].astype(jnp.float32) * factor[s, :, h : h + 1]
        out_ref[:, span] = value.astype(jnp.bfloat16)


def combine(parts, heads):
    rows = parts.shape[1]
    return pl.pallas_call(
        functools.partial(combine_kernel, heads=heads),
        out_shape=jax.ShapeDtypeStruct((rows, heads * LANES), jnp.bfloat16),
        name="combine",
    )(parts)


def project_kernel(x_ref, w_ref, out_ref):
    out_ref[0] = jnp.dot(x_ref[...], w_ref[...], preferred_element_type=jnp.float32).astype(
        jnp.bfloat16
    )


def project(x, weight, pieces):
    rows, depth = x.shape
    columns = weight.shape[1]
    piece = columns // pieces
    if piece % LANES:
        terms = jnp.dot(x, weight, preferred_element_type=jnp.float32).astype(jnp.bfloat16)
        return terms.reshape(rows, pieces, piece).transpose(1, 0, 2)
    return pl.pallas_call(
        project_kernel,
        grid=(pieces,),
        out_shape=jax.ShapeDtypeStruct((pieces, rows, piece), jnp.bfloat16),
        in_specs=[
            pl.BlockSpec((rows, depth), lambda i: (0, 0)),
            pl.BlockSpec((depth, piece), lambda i: (0, i)),
        ],
        out_specs=pl.BlockSpec((1, rows, piece), lambda i: (i, 0, 0)),
        name="project",
    )(x, weight)


def spread(x, axis):
    count = lax.axis_size(axis)
    copies = jnp.broadcast_to(x[None], (count,) + x.shape)
    out = lax.all_to_all(copies, axis, split_axis=0, concat_axis=0, tiled=True)
    return out.reshape((count * x.shape[0],) + x.shape[1:])


def pack_request(queries, lengths, page_table):
    rows, heads, head_size = queries.shape
    high = page_table >> 8
    low = page_table & 255
    pair = jnp.stack([lengths >> 8, lengths & 255], axis=1)
    pad = [
        jnp.pad(part.astype(jnp.bfloat16), ((0, 0), (0, LANES - part.shape[1])))
        for part in (high, low, pair)
    ]
    return jnp.concatenate([queries.reshape(rows, heads * head_size)] + pad, axis=1)


def on_device(
    queries,
    k_codes,
    value_quantized_codes,
    key_page_scale,
    value_page_scale,
    lengths,
    page_table,
    out_weight,
):
    pages, tokens, kv, head_size = k_codes.shape
    rows, heads, _ = queries.shape
    gathered = spread(pack_request(queries, lengths, page_table), "req")
    offset = (lax.axis_index("req") * pages).astype(jnp.int32).reshape(1)
    partial = attend(
        gathered,
        offset,
        k_codes.reshape(pages * tokens * kv, head_size),
        value_quantized_codes.reshape(pages * tokens * kv, head_size),
        key_page_scale.T,
        value_page_scale.T,
        heads,
        kv,
        tokens,
    )
    sources = lax.axis_size("req")
    parts = lax.all_to_all(
        partial.reshape(sources, rows, partial.shape[1]),
        "req",
        split_axis=0,
        concat_axis=0,
        tiled=True,
    )
    attention = spread(combine(parts, heads), "req")
    terms = project(attention, out_weight, lax.axis_size("head"))
    terms = lax.all_to_all(terms, "head", split_axis=0, concat_axis=0, tiled=True)
    return jnp.sum(terms.astype(jnp.float32), axis=0).astype(jnp.bfloat16)


def solution(mesh):
    in_specs = (
        P("req", "head", None),
        P("req", None, "head", None),
        P("req", None, "head", None),
        P("req", "head"),
        P("req", "head"),
        P("req"),
        P("req", None),
        P("head", "req"),
    )
    out_specs = P(None, ("req", "head"))
    return jax.shard_map(
        on_device, mesh=mesh, in_specs=in_specs, out_specs=out_specs, check_vma=False
    )
```

time: 247 us -> 104 us (0.42)
  local copies, waits for them, and re-layouts: 88.3 us -> 3.55 us
  matrix products: 44.7 us -> 0 us
  Pallas kernels: 0 us -> 41.6 us
  waiting for transfers between devices: 33.1 us -> 10.8 us
  other arithmetic: 17.9 us -> 2.05 us
  between operations: 14.4 us -> 0.03 us
  starting transfers between devices: 11.7 us -> 5.2 us
  blocking collectives: 36.5 us -> 40.2 us
    scatter x1 -> x0, local copies, waits for them, and re-layouts: 60.3 us -> none  [locate_pages(): jnp.zeros((pages_here,), jnp.int32).at[target].set(entry_code, mode='drop')]
    dot_general x7 -> x0, matrix products: 44.7 us -> none  [the longest x2 14.5 us: split_product(): jnp.dot(member_b, low_part, preferred_element_type=jnp.float32)]
    pallas_call x0 -> x3, Pallas kernels: none -> 41.6 us  [the longest x1 34.9 us: attend(): pl.pallas_call(functools.partial(attend_kernel, heads=heads, kv=kv, token...]
    all_to_all x0 -> x3, blocking collectives: none -> 40.2 us  [the longest x1 14.2 us: on_device(): lax.all_to_all(partial.reshape(sources, rows, partial.shape[1]), 'req', s...]
    all_gather x3 -> x0, blocking collectives: 27 us -> none  [the longest x1 9.51 us: on_device(): every_query = lax.all_gather(queries, 'req', axis=0, tiled=True)]
    reduce_scatter x1 -> x0, waiting for transfers between devices: 20.4 us -> none  [on_device(): lax.psum_scatter(terms.astype(jnp.bfloat16), 'head', scatter_dimension=1,...]
    gather x4 -> x0, local copies, waits for them, and re-layouts: 18 us -> none  [the longest x1 8.47 us: on_device(): every_query[owners]]
    unnamed x1 -> x0, blocking collectives: 9.49 us -> none
  transfers between devices with their start and end apart: 4 -> 1, of which waited for: 2 -> 1; matrix products, arithmetic and copies ran while one was open for 21% -> 0% of each run, Pallas kernels for 0% -> 0%
where the time goes in v1:
time: 104 us; the launch traced here: 103 us
  Pallas kernels  41.6 us (40%)
  blocking collectives  40.2 us (39%)
  waiting for transfers between devices  10.8 us (10%)
  starting transfers between devices  5.2 us (5%)
  local copies, waits for them, and re-layouts  3.55 us (3%)
  other arithmetic  2.05 us (2%)
    pallas_call x1, Pallas kernels, attend(): pl.pallas_call(functools.partial(attend_kernel, heads=heads, kv=kv, token...  34.9 us
    all_to_all x1, blocking collectives, on_device(): lax.all_to_all(partial.reshape(sources, rows, partial.shape[1]), 'req', s...  14.2 us
    all_to_all x1, blocking collectives, on_device(): lax.all_to_all(terms, 'head', split_axis=0, concat_axis=0, tiled=True)  13.2 us
    all_to_all x1, blocking collectives, spread(): out = lax.all_to_all(copies, axis, split_axis=0, concat_axis=0, tiled=True)  12.8 us
    all_to_all x1, waiting for transfers between devices, spread(): out = lax.all_to_all(copies, axis, split_axis=0, concat_axis=0, tiled=True)  10.8 us
    all_to_all x1, starting transfers between devices, spread(): out = lax.all_to_all(copies, axis, split_axis=0, concat_axis=0, tiled=True)  5.2 us
    pallas_call x1, Pallas kernels, project(): pl.pallas_call(project_kernel, grid=(pieces,), out_shape=jax.ShapeDtypeSt...  4.54 us
    pallas_call x1, Pallas kernels, combine(): pl.pallas_call(functools.partial(combine_kernel, heads=heads), out_shape=...  2.23 us
  transfers between devices with their start and end apart: 1, of which 1 were waited for; matrix products, arithmetic and copies ran while one was open for 0% of the time, Pallas kernels for 0%

profile of v1, /device:TPU:0, one launch (start us, length us, event | category | flops | bytes accessed | tf_op | source)
XLA Modules:
  0.0 103.4 jit_solution(14765358682718722077)
XLA Ops:
  0.0 0.7 convert_bitcast_fusion.1
  0.7 0.1 copy.10
  0.8 0.7 shift-right-arithmetic_convert_fusion
  1.5 0.9 copy.13
  2.4 0.9 broadcast_in_dim.4
  3.2 5.2 %all-to-all-start = ((bf16[8,16,2432]{2,1,0:T(8,128)(2,1)}), bf16[8,16,2432]{2,1,0:T(8,128)(2,1)S(1)}, u32[]{:S(2)}, u32[]{:S(2)}) async-start(bf16[8,16,2432]{2,1,0:T(8,128)(2,1)} %broadcast_in_dim.4), calls=%async_computation | async-start | bytes 1245184 | tf_op jit(solution)/shard_map/all_to_all | solution.py:311
  8.4 10.8 %all-to-all-done = bf16[8,16,2432]{2,1,0:T(8,128)(2,1)S(1)} async-done(((bf16[8,16,2432]{2,1,0:T(8,128)(2,1)}), bf16[8,16,2432]{2,1,0:T(8,128)(2,1)S(1)}, u32[]{:S(2)}, u32[]{:S(2)}) %all-to-all-start) | async-done | bytes 622624 | tf_op jit(solution)/shard_map/all_to_all | solution.py:311
  19.2 0.0 copy-start
  19.2 0.8 copy-done
  20.0 34.9 %attend.1 = bf16[128,2176]{1,0:T(8,128)(2,1)} custom-call(s32[1]{0:T(128)} %bitcast.offset_ref, bf16[128,2432]{1,0:T(8,128)(2,1)} %bitcast.18, f32[2,1024]{1,0:T(2,128)} %bitcast.23, f32[2,1024]{1,0:T(2,128)} %bitcast.24, bf16[32768,128]{1,0:T(8,128)(2,1)} %bitcast.16, bf16[32768,128]{1,0:T(8,128)(2,1)} %bitcast.17), custom_call_target="tpu_custom_call" | custom-call | tf_op jit(solution)/shard_map/attend/pallas_call | solution.py:233
  54.9 14.2 %all_to_all.20.in_ref = bf16[8,16,2176]{2,1,0:T(8,128)(2,1)} all-to-all(bf16[8,16,2176]{2,1,0:T(8,128)(2,1)} %bitcast.19), channel_id=1, replica_groups=mesh['req'=8,'head'=4] {'req'}, dimensions={0} | all-to-all | bytes 1114112 | tf_op jit(solution)/shard_map/all_to_all | solution.py:353
  69.1 2.2 %combine.1 = bf16[16,2048]{1,0:T(8,128)(2,1)} custom-call(bf16[8,16,2176]{2,1,0:T(8,128)(2,1)} %all_to_all.20.in_ref), custom_call_target="tpu_custom_call" | custom-call | tf_op jit(solution)/shard_map/combine/pallas_call | solution.py:275
  71.4 0.9 broadcast_in_dim.5
  72.3 12.8 %all_to_all.21 = bf16[8,16,2048]{2,1,0:T(8,128)(2,1)} all-to-all(bf16[8,16,2048]{2,1,0:T(8,128)(2,1)S(1)} %broadcast_in_dim.5), channel_id=1, replica_groups=mesh['req'=8,'head'=4] {'req'}, dimensions={0} | all-to-all | bytes 1048576 | tf_op jit(solution)/shard_map/all_to_all | solution.py:311
  85.1 4.5 %project.1 = bf16[4,128,256]{2,1,0:T(8,128)(2,1)} custom-call(bf16[128,2048]{1,0:T(8,128)(2,1)} %bitcast.20, bf16[2048,1024]{1,0:T(8,128)(2,1)} %w_ref.1), custom_call_target="tpu_custom_call" | custom-call | tf_op jit(solution)/shard_map/project/pallas_call | solution.py:295
  89.6 13.2 %all_to_all.22 = bf16[4,128,256]{2,1,0:T(8,128)(2,1)S(1)} all-to-all(bf16[4,128,256]{2,1,0:T(8,128)(2,1)} %project.1), channel_id=1, replica_groups=mesh['req'=8,'head'=4] {'head'}, dimensions={0} | all-to-all | bytes 524288 | tf_op jit(solution)/shard_map/all_to_all | solution.py:362
  102.8 0.7 reduce_sum.12
  (2 shorter events, 0.0 us)
Async XLA Ops:
  3.2 16.0 %all-to-all-start = ((bf16[8,16,2432]{2,1,0:T(8,128)(2,1)}), bf16[8,16,2432]{2,1,0:T(8,128)(2,1)S(1)}, u32[]{:S(2)}, u32[]{:S(2)}) async-start(bf16[8,16,2432]{2,1,0:T(8,128)(2,1)} %broadcast_in_dim.4), calls=%async_computation | async-start | bytes 1245184 | tf_op jit(solution)/shard_map/all_to_all | solution.py:311
  19.2 0.8 copy-start
